TPU v7x, 256 devices: a whole 4x4x8 slice. The times are simulated.
256 devices in a mesh: seq: 64 (over x, z, core), grp: 4 (over y).
Axes of the slice: x: 4, y: 4, z: 8, core: 2. Of those that a mesh axis runs over, the one named last changes fastest.
Arguments:
- delta_codes: int32 [16, 16, 16384, 128], P('grp', None, 'seq'), may hold values from -63 to 63, as said below
- scale_index: int32 [16, 16, 1024], P('grp', None, 'seq'), may hold values from 0 to 15
- anchor_codes: int32 [16, 16, 128], P('grp'), may hold values from -8 to 7
- scale_table: float32 [16, 128], replicated, may hold values from 5e-05 to 0.0005
- anchor_scale: float32 [128], replicated, may hold values from 0.0001 to 0.001
Outputs:
- decode_cache: bfloat16 [4, 64, 16384, 128], P('grp', 'seq')
Inputs may be any that keep to these rules, and one draw needn't show every extreme that they name: `delta_codes`: for every sequence, head and channel, the running sum of the codes from the sequence's first token lies in -32 .. 31 after every token, and in -2 .. 1 after the last token of each group of 16 tokens.
All inputs are finite; a program needn't handle non-finite values.
Results may differ from a plain program's by a relative error of at most 0.001.
Values may be sent and summed in bfloat16 or wider, within the bound.
A program may use at most 128 MiB of HBM per device.

v0:
```python
import jax
import jax.numpy as jnp
from jax import lax
from jax.sharding import PartitionSpec as P


def lookup_scales(scale_ids, scale_table):
    levels = scale_table.shape[0]
    onehot = (scale_ids[..., None] == jnp.arange(levels, dtype=jnp.int32)).astype(jnp.float32)
    flat = jnp.dot(
        onehot.reshape(-1, levels),
        scale_table,
        precision=lax.Precision.HIGHEST,
        preferred_element_type=jnp.float32,
    )
    return flat.reshape(scale_ids.shape + (scale_table.shape[1],))


def dequantize(code_vals, scale_ids, scale_table):
    head_dim = code_vals.shape[-1]
    steps_len = code_vals.shape[-2]
    groups = scale_ids.shape[-1]
    scales = lookup_scales(scale_ids, scale_table)
    lead_dims = code_vals.shape[:-2]
    shaped = code_vals.astype(jnp.float32).reshape(
        lead_dims + (groups, steps_len // groups, head_dim)
    )
    return (shaped * scales[..., :, None, :]).reshape(code_vals.shape)


def block_prefix(deltas):
    tok_len = deltas.shape[1]
    lower_ones = (jnp.arange(tok_len)[:, None] >= jnp.arange(tok_len)[None, :]).astype(jnp.float32)
    return jnp.einsum("tu,ruc->rtc", lower_ones, deltas, precision=lax.Precision.HIGHEST)


def finish_rows(prefix_rows, totals, seq_count):
    strict = (jnp.arange(seq_count)[:, None] > jnp.arange(seq_count)[None, :]).astype(jnp.float32)
    carried = jnp.einsum("ij,rjc->ric", strict, totals, precision=lax.Precision.HIGHEST)
    row_count, length, head_dim = prefix_rows.shape
    shaped = (
        prefix_rows.reshape(row_count, seq_count, length // seq_count, head_dim)
        + carried[:, :, None, :]
    )
    return shaped.astype(jnp.bfloat16).reshape(row_count, length, head_dim)


def on_device(delta_codes, scale_index, anchor_codes, scale_table, anchor_scale):
    seq_count = lax.axis_size("seq")
    seq_local, kv_heads, tok_dev, head_dim = delta_codes.shape
    packed = (
        delta_codes.astype(jnp.bfloat16),
        scale_index.astype(jnp.bfloat16),
        anchor_codes.astype(jnp.bfloat16),
    )
    sectioned = (
        lax.all_to_all(packed[0], "grp", split_axis=1, concat_axis=0, tiled=True),
        lax.all_to_all(packed[1], "grp", split_axis=1, concat_axis=0, tiled=True),
        lax.all_to_all(packed[2], "grp", split_axis=1, concat_axis=0, tiled=True),
    )
    code_rows = sectioned[0].reshape(-1, tok_dev, head_dim)
    id_rows = sectioned[1].reshape(code_rows.shape[0], -1)
    anchor_rows = sectioned[2].reshape(code_rows.shape[0], head_dim)
    moved = (
        lax.all_to_all(code_rows, "seq", split_axis=0, concat_axis=1, tiled=True),
        lax.all_to_all(id_rows, "seq", split_axis=0, concat_axis=1, tiled=True),
    )
    row_count = moved[0].shape[0]
    start = lax.axis_index("seq") * row_count
    my_anchor = lax.dynamic_slice_in_dim(anchor_rows, start, row_count, 0)
    anchor_vals = my_anchor.astype(jnp.float32) * anchor_scale
    deltas = dequantize(moved[0], moved[1].astype(jnp.int32), scale_table)
    prefix = block_prefix(deltas.reshape(-1, tok_dev, head_dim)).reshape(
        row_count, seq_count, tok_dev, head_dim
    )
    totals = prefix[:, :, -1, :]
    prefix_rows = (prefix + anchor_vals[:, None, None, :]).reshape(row_count, -1, head_dim)
    result = finish_rows(prefix_rows, totals, seq_count)
    return result[None]


def solution(mesh):
    placed = (P("grp", None, "seq", None), P("grp", None, "seq"), P("grp", None, None), P(), P())
    return jax.shard_map(
        on_device,
        mesh=mesh,
        in_specs=placed,
        out_specs=P("grp", "seq", None, None),
        check_vma=False,
    )
```

profile of v0, /device:TPU:1, one launch (start us, length us, event | category | flops | bytes accessed | tf_op | source)
XLA Modules:
  0.0 227.8 jit_solution(3346207164019680870)
XLA Ops:
  0.0 0.8 fusion.8
  0.8 0.1 reshape.92
  0.9 8.9 %all_to_all.67 = bf16[4,2,128]{2,1,0:T(2,128)(2,1)S(1)} all-to-all(bf16[4,2,128]{2,1,0:T(2,128)(2,1)S(1)} %reshape.92), channel_id=1, replica_groups=mesh['seq'=64,'grp'=4] {'grp'}, dimensions={0} | all-to-all | bytes 4096 | tf_op jit(solution)/shard_map/all_to_all | solution.py:58
  9.8 0.1 reshape.93
  9.9 0.6 copy.17
  10.5 13.6 %all-to-all-start.3 = ((bf16[64,1,16]{2,1,0:T(2,128)(2,1)}), bf16[64,1,16]{2,1,0:T(2,128)(2,1)S(1)}, u32[]{:S(2)}, u32[]{:S(2)}) async-start(bf16[64,1,16]{2,1,0:T(2,128)(2,1)} %copy.17), calls=%async_computation.3 | async-start | bytes 65536 | tf_op jit(solution)/shard_map/all_to_all | solution.py:66
  24.1 6.4 %copy_convert_fusion = bf16[4,16,256,128]{3,2,0,1:T(8,128)(2,1)} fusion(s32[4,16,256,128]{3,2,1,0:T(8,128)} %param.5), kind=kLoop, calls=%fused_computation.4 | loop fusion | flops 2097152 | bytes 12582912 | tf_op jit(solution)/shard_map/convert_element_type | solution.py:52
  30.5 2.9 %all-to-all-done.3 = bf16[64,1,16]{2,1,0:T(2,128)(2,1)S(1)} async-done(((bf16[64,1,16]{2,1,0:T(2,128)(2,1)}), bf16[64,1,16]{2,1,0:T(2,128)(2,1)S(1)}, u32[]{:S(2)}, u32[]{:S(2)}) %all-to-all-start.3) | async-done | bytes 2080 | tf_op jit(solution)/shard_map/all_to_all | solution.py:66
  33.4 4.8 %all-to-all-start = ((bf16[4,16,256,128]{3,2,0,1:T(8,128)(2,1)}), bf16[4,16,256,128]{3,2,0,1:T(8,128)(2,1)}, u32[]{:S(2)}, u32[]{:S(2)}) async-start(bf16[4,16,256,128]{3,2,0,1:T(8,128)(2,1)} %copy_convert_fusion), calls=%async_computation | async-start | bytes 8388608 | tf_op jit(solution)/shard_map/all_to_all | solution.py:57
  38.3 0.6 copy_convert_fusion.1
  38.9 47.7 %all-to-all-done = bf16[4,16,256,128]{3,2,0,1:T(8,128)(2,1)} async-done(((bf16[4,16,256,128]{3,2,0,1:T(8,128)(2,1)}), bf16[4,16,256,128]{3,2,0,1:T(8,128)(2,1)}, u32[]{:S(2)}, u32[]{:S(2)}) %all-to-all-start) | async-done | bytes 4194336 | tf_op jit(solution)/shard_map/all_to_all | solution.py:57
  86.6 3.2 %all-to-all-start.4 = ((bf16[4,16,128]{2,0,1:T(4,128)(2,1)}), bf16[4,16,128]{2,0,1:T(4,128)(2,1)S(1)}, u32[]{:S(2)}, u32[]{:S(2)}) async-start(bf16[4,16,128]{2,0,1:T(4,128)(2,1)} %copy_convert_fusion.1), calls=%async_computation.4 | async-start | bytes 32768 | tf_op jit(solution)/shard_map/all_to_all | solution.py:59
  89.8 4.7 %copy.14 = bf16[4,4,4,256,128]{4,3,2,0,1:T(8,128)(2,1)} copy(bf16[4,4,4,256,128]{4,3,0,2,1:T(8,128)(2,1)} %bitcast) | data formatting | bytes 8388608 | tf_op jit(solution)/shard_map/all_to_all | solution.py:57
  94.6 9.3 %all-to-all-start.1 = ((bf16[64,256,128]{2,1,0:T(8,128)(2,1)}), bf16[64,256,128]{2,1,0:T(8,128)(2,1)}, u32[]{:S(2)}, u32[]{:S(2)}) async-start(bf16[64,256,128]{2,1,0:T(8,128)(2,1)} %bitcast.47), calls=%async_computation.1 | async-start | bytes 8388608 | tf_op jit(solution)/shard_map/all_to_all | solution.py:65
  103.9 0.1 convert_reduce_fusion
  104.1 0.5 fusion.2
  104.6 95.1 %all-to-all-done.1 = bf16[64,256,128]{2,1,0:T(8,128)(2,1)} async-done(((bf16[64,256,128]{2,1,0:T(8,128)(2,1)}), bf16[64,256,128]{2,1,0:T(8,128)(2,1)}, u32[]{:S(2)}, u32[]{:S(2)}) %all-to-all-start.1) | async-done | bytes 4194336 | tf_op jit(solution)/shard_map/all_to_all | solution.py:65
  199.8 0.5 mul.16
  200.3 6.7 %bitcast_multiply_fusion = f32[64,256,128]{2,1,0:T(8,128)} fusion(bf16[64,256,128]{2,1,0:T(8,128)(2,1)} %all-to-all-done.1, f32[64,256,128]{2,1,0:T(8,128)S(1)} %bitcast.46), kind=kLoop, calls=%fused_computation.3 | loop fusion | flops 4194304 | bytes 20971520 | tf_op jit(solution)/shard_map/mul | solution.py:28
  207.0 9.4 %fusion.5 = f32[64,128,256]{2,1,0:T(8,128)S(1)} fusion(f32[64,256,128]{2,1,0:T(8,128)} %bitcast_multiply_fusion), kind=kOutput, calls=%fused_computation.12 | convolution fusion | flops 6442516480 | bytes 16777216 | tf_op jit(solution)/shard_map/tu,ruc->rtc/dot_general | solution.py:34
  216.4 2.2 slice_reduce_fusion
  218.7 0.1 convolution_bitcast_fusion
  218.8 2.6 %fusion.1 = bf16[64,256,128]{1,2,0:T(8,128)(2,1)} fusion(f32[64,128,256]{2,1,0:T(8,128)S(1)} %fusion.5, f32[64,128]{1,0:T(8,128)S(1)} %convolution_bitcast_fusion, f32[128]{0:T(128)S(1)} %fusion.7), kind=kLoop, calls=%fused_computation.2 | loop fusion | flops 6291456 | bytes 12616192 | tf_op jit(solution)/shard_map/convert_element_type | solution.py:45
  221.5 6.4 %copy.21 = bf16[64,256,128]{2,1,0:T(8,128)(2,1)} copy(bf16[64,256,128]{1,2,0:T(8,128)(2,1)} %fusion.1) | data formatting | bytes 8388608 | tf_op jit(solution)/shard_map/convert_element_type | solution.py:45
  (11 shorter events, 0.1 us)
Async XLA Ops:
  0.0 104.1 %copy-start = (f32[16,128]{1,0:T(8,128)S(1)}, f32[16,128]{1,0:T(8,128)}, u32[]{:S(2)}) copy-start(f32[16,128]{1,0:T(8,128)} %param.8) | copy-start | bytes 24580
  10.5 22.9 %all-to-all-start.3 = ((bf16[64,1,16]{2,1,0:T(2,128)(2,1)}), bf16[64,1,16]{2,1,0:T(2,128)(2,1)S(1)}, u32[]{:S(2)}, u32[]{:S(2)}) async-start(bf16[64,1,16]{2,1,0:T(2,128)(2,1)} %copy.17), calls=%async_computation.3 | async-start | bytes 65536 | tf_op jit(solution)/shard_map/all_to_all | solution.py:66
  24.1 14.2 %copy-start.1 = (s32[4,16,128]{2,1,0:T(8,128)S(1)}, s32[4,16,128]{2,1,0:T(8,128)}, u32[]{:S(2)}) copy-start(s32[4,16,128]{2,1,0:T(8,128)} %param.7) | copy-start | bytes 98308
  33.4 53.1 %all-to-all-start = ((bf16[4,16,256,128]{3,2,0,1:T(8,128)(2,1)}), bf16[4,16,256,128]{3,2,0,1:T(8,128)(2,1)}, u32[]{:S(2)}, u32[]{:S(2)}) async-start(bf16[4,16,256,128]{3,2,0,1:T(8,128)(2,1)} %copy_convert_fusion), calls=%async_computation | async-start | bytes 8388608 | tf_op jit(solution)/shard_map/all_to_all | solution.py:57
  86.6 8.0 %all-to-all-start.4 = ((bf16[4,16,128]{2,0,1:T(4,128)(2,1)}), bf16[4,16,128]{2,0,1:T(4,128)(2,1)S(1)}, u32[]{:S(2)}, u32[]{:S(2)}) async-start(bf16[4,16,128]{2,0,1:T(4,128)(2,1)} %copy_convert_fusion.1), calls=%async_computation.4 | async-start | bytes 32768 | tf_op jit(solution)/shard_map/all_to_all | solution.py:59
  89.8 14.8 %copy-start.2 = (f32[128]{0:T(128)S(1)}, f32[128]{0:T(128)}, u32[]{:S(2)}) copy-start(f32[128]{0:T(128)} %param.9) | copy-start | bytes 1540
  94.6 105.2 %all-to-all-start.1 = ((bf16[64,256,128]{2,1,0:T(8,128)(2,1)}), bf16[64,256,128]{2,1,0:T(8,128)(2,1)}, u32[]{:S(2)}, u32[]{:S(2)}) async-start(bf16[64,256,128]{2,1,0:T(8,128)(2,1)} %bitcast.47), calls=%async_computation.1 | async-start | bytes 8388608 | tf_op jit(solution)/shard_map/all_to_all | solution.py:65
where the time goes:
time: 228 us
  waiting for transfers between devices  146 us (64%)
  starting transfers between devices  31 us (14%)
  other arithmetic  17.3 us (8%)
  local copies, waits for them, and re-layouts  14.8 us (6%)
  matrix products  9.98 us (4%)
  blocking collectives  8.93 us (4%)
    all_to_all x1, waiting for transfers between devices, on_device(): lax.all_to_all(code_rows, 'seq', split_axis=0, concat_axis=1, tiled=True)  95.1 us
    all_to_all x1, waiting for transfers between devices, on_device(): lax.all_to_all(packed[0], 'grp', split_axis=1, concat_axis=0, tiled=True)  47.7 us
    all_to_all x1, starting transfers between devices, on_device(): lax.all_to_all(id_rows, 'seq', split_axis=0, concat_axis=1, tiled=True)  13.6 us
    dot_general x1, matrix products, block_prefix(): jnp.einsum('tu,ruc->rtc', lower_ones, deltas, precision=lax.Precision.HIG...  9.38 us
    all_to_all x1, starting transfers between devices, on_device(): lax.all_to_all(code_rows, 'seq', split_axis=0, concat_axis=1, tiled=True)  9.35 us
    all_to_all x1, blocking collectives, on_device(): lax.all_to_all(packed[1], 'grp', split_axis=1, concat_axis=0, tiled=True)  8.93 us
    mul x1, other arithmetic, dequantize(): return (shaped * scales[..., :, None, :]).reshape(code_vals.shape)  6.73 us
    convert_element_type x1, other arithmetic, on_device(): delta_codes.astype(jnp.bfloat16)  6.38 us
  transfers between devices with their start and end apart: 4, of which 3 were waited for; matrix products, arithmetic and copies ran while one was open for 5% of the time, Pallas kernels for 0%

commit v1 on v0

--- a/solution.py
+++ b/solution.py
@@ -62,7 +62,12 @@
     id_rows = sectioned[1].reshape(code_rows.shape[0], -1)
     anchor_rows = sectioned[2].reshape(code_rows.shape[0], head_dim)
     moved = (
-        lax.all_to_all(code_rows, "seq", split_axis=0, concat_axis=1, tiled=True),
+        jnp.concatenate(
+            lax.all_to_all(
+                jnp.stack(jnp.split(code_rows, lax.axis_size("seq"), axis=0)), "seq", 0, 0
+            ),
+            axis=1,
+        ),
         lax.all_to_all(id_rows, "seq", split_axis=0, concat_axis=1, tiled=True),
     )
     row_count = moved[0].shape[0]

time: 228 us -> 259 us (1.14)
  local copies, waits for them, and re-layouts: 14.8 us -> 55 us
  blocking collectives: 8.93 us -> 0 us
  starting transfers between devices: 31 us -> 38.6 us
  other arithmetic: 17.3 us -> 10.6 us
    unnamed x8 -> x73, local copies, waits for them, and re-layouts: 0.19 us -> 41.2 us
    all_to_all x1 -> x0, blocking collectives: 8.93 us -> none  [on_device(): lax.all_to_all(packed[1], 'grp', split_axis=1, concat_axis=0, tiled=True)]
    all_to_all x1 -> x2, starting transfers between devices: 9.35 us -> 16.7 us  [the longest x1 11.7 us: on_device(): lax.all_to_all(jnp.stack(jnp.split(code_rows, lax.axis_size('seq'), axis=...]
    mul x1 -> x0, other arithmetic: 6.73 us -> none  [dequantize(): return (shaped * scales[..., :, None, :]).reshape(code_vals.shape)]
    all_to_all x1, waiting for transfers between devices: 2.92 us -> 0.01 us  [on_device(): lax.all_to_all(id_rows, 'seq', split_axis=0, concat_axis=1, tiled=True)]
    all_to_all x1, waiting for transfers between devices: 0.01 us -> 2.7 us  [on_device(): lax.all_to_all(packed[2], 'grp', split_axis=1, concat_axis=0, tiled=True)]
    all_to_all x1 -> x2, waiting for transfers between devices: 95.1 us -> 95.1 us  [the longest x1 95.1 us: on_device(): lax.all_to_all(jnp.stack(jnp.split(code_rows, lax.axis_size('seq'), axis=...]
  transfers between devices with their start and end apart: 4 -> 5, of which waited for: 3 -> 3; matrix products, arithmetic and copies ran while one was open for 5% -> 20% of each run, Pallas kernels for 0% -> 0%
where the time goes in v1:
time: 259 us
  waiting for transfers between devices  144 us (56%)
  local copies, waits for them, and re-layouts  55 us (21%)
  starting transfers between devices  38.6 us (15%)
  other arithmetic  10.6 us (4%)
  matrix products  10.1 us (4%)
    all_to_all x1, waiting for transfers between devices, on_device(): lax.all_to_all(jnp.stack(jnp.split(code_rows, lax.axis_size('seq'), axis=...  95.1 us
    all_to_all x1, waiting for transfers between devices, on_device(): lax.all_to_all(packed[0], 'grp', split_axis=1, concat_axis=0, tiled=True)  46.2 us
    unnamed x73, local copies, waits for them, and re-layouts  41.2 us
    all_to_all x1, starting transfers between devices, on_device(): lax.all_to_all(id_rows, 'seq', split_axis=0, concat_axis=1, tiled=True)  13.8 us
    all_to_all x1, starting transfers between devices, on_device(): lax.all_to_all(jnp.stack(jnp.split(code_rows, lax.axis_size('seq'), axis=...  11.7 us
    dot_general x1, matrix products, block_prefix(): jnp.einsum('tu,ruc->rtc', lower_ones, deltas, precision=lax.Precision.HIG...  9.5 us
    convert_element_type x1, other arithmetic, on_device(): delta_codes.astype(jnp.bfloat16)  6.37 us
    convert_element_type x1, local copies, waits for them, and re-layouts, finish_rows(): return shaped.astype(jnp.bfloat16).reshape(row_count, length, head_dim)  6.35 us
  transfers between devices with their start and end apart: 5, of which 3 were waited for; matrix products, arithmetic and copies ran while one was open for 20% of the time, Pallas kernels for 0%

profile of v1, /device:TPU:1, one launch (start us, length us, event | category | flops | bytes accessed | tf_op | source)
XLA Modules:
  0.0 258.6 jit_solution(14411382428957409668)
XLA Ops:
  0.0 0.8 fusion.9
  0.8 0.7 reshape.93
  1.5 5.0 %all-to-all-start.2 = ((bf16[4,2,128]{2,1,0:T(2,128)(2,1)}), bf16[4,2,128]{2,1,0:T(2,128)(2,1)S(1)}, u32[]{:S(2)}, u32[]{:S(2)}) async-start(bf16[4,2,128]{2,1,0:T(2,128)(2,1)} %reshape.93), calls=%async_computation.2 | async-start | bytes 4096 | tf_op jit(solution)/shard_map/all_to_all | solution.py:58
  6.5 6.4 %copy_convert_fusion = bf16[4,16,256,128]{3,2,0,1:T(8,128)(2,1)} fusion(s32[4,16,256,128]{3,2,1,0:T(8,128)} %param.5), kind=kLoop, calls=%fused_computation.5 | loop fusion | flops 2097152 | bytes 12582912 | tf_op jit(solution)/shard_map/convert_element_type | solution.py:52
  12.9 5.0 %all-to-all-start = ((bf16[4,16,256,128]{3,2,0,1:T(8,128)(2,1)}), bf16[4,16,256,128]{3,2,0,1:T(8,128)(2,1)}, u32[]{:S(2)}, u32[]{:S(2)}) async-start(bf16[4,16,256,128]{3,2,0,1:T(8,128)(2,1)} %copy_convert_fusion), calls=%async_computation | async-start | bytes 8388608 | tf_op jit(solution)/shard_map/all_to_all | solution.py:57
  18.6 0.6 copy.144
  19.2 46.2 %all-to-all-done = bf16[4,16,256,128]{3,2,0,1:T(8,128)(2,1)} async-done(((bf16[4,16,256,128]{3,2,0,1:T(8,128)(2,1)}), bf16[4,16,256,128]{3,2,0,1:T(8,128)(2,1)}, u32[]{:S(2)}, u32[]{:S(2)}) %all-to-all-start) | async-done | bytes 4194336 | tf_op jit(solution)/shard_map/all_to_all | solution.py:57
  65.4 13.8 %all-to-all-start.3 = ((bf16[64,1,16]{2,1,0:T(2,128)(2,1)}), bf16[64,1,16]{2,1,0:T(2,128)(2,1)S(1)}, u32[]{:S(2)}, u32[]{:S(2)}) async-start(bf16[64,1,16]{2,1,0:T(2,128)(2,1)} %copy.144), calls=%async_computation.3 | async-start | bytes 65536 | tf_op jit(solution)/shard_map/all_to_all | solution.py:71
  79.2 2.5 copy.140
  81.6 0.7 constant_dynamic-update-slice_fusion.63
  82.3 1.1 constant_dynamic-update-slice_fusion.62
  84.1 0.6 constant_dynamic-update-slice_fusion.60
  85.3 0.6 constant_dynamic-update-slice_fusion.58
  86.6 0.6 constant_dynamic-update-slice_fusion.56
  121.5 0.6 constant_dynamic-update-slice_fusion.1
  122.1 3.2 %all-to-all-start.4 = ((bf16[4,16,128]{2,0,1:T(4,128)(2,1)}), bf16[4,16,128]{2,0,1:T(4,128)(2,1)S(1)}, u32[]{:S(2)}, u32[]{:S(2)}) async-start(bf16[4,16,128]{2,0,1:T(4,128)(2,1)} %copy_convert_fusion.1), calls=%async_computation.4 | async-start | bytes 32768 | tf_op jit(solution)/shard_map/all_to_all | solution.py:59
  125.4 1.5 constant_dynamic-update-slice_fusion
  126.9 2.7 %all-to-all-done.4 = bf16[4,16,128]{2,0,1:T(4,128)(2,1)S(1)} async-done(((bf16[4,16,128]{2,0,1:T(4,128)(2,1)}), bf16[4,16,128]{2,0,1:T(4,128)(2,1)S(1)}, u32[]{:S(2)}, u32[]{:S(2)}) %all-to-all-start.4) | async-done | bytes 16416 | tf_op jit(solution)/shard_map/all_to_all | solution.py:59
  129.6 11.7 %all-to-all-start.1 = ((bf16[64,1,256,128]{3,2,1,0:T(8,128)(2,1)}), bf16[64,1,256,128]{3,2,1,0:T(8,128)(2,1)}, u32[]{:S(2)}, u32[]{:S(2)}) async-start(bf16[64,1,256,128]{3,2,1,0:T(8,128)(2,1)} %constant_dynamic-update-slice_fusion), calls=%async_computation.1 | async-start | bytes 8388608 | tf_op jit(solution)/shard_map/all_to_all | solution.py:66
  142.0 95.1 %all-to-all-done.1 = bf16[64,1,256,128]{3,2,1,0:T(8,128)(2,1)} async-done(((bf16[64,1,256,128]{3,2,1,0:T(8,128)(2,1)}), bf16[64,1,256,128]{3,2,1,0:T(8,128)(2,1)}, u32[]{:S(2)}, u32[]{:S(2)}) %all-to-all-start.1) | async-done | bytes 4194336 | tf_op jit(solution)/shard_map/all_to_all | solution.py:66
  237.6 9.5 %fusion = f32[64,128,256]{2,1,0:T(8,128)S(1)} fusion(f32[64,256,128]{2,1,0:T(8,128)S(1)} %bitcast.307, bf16[64,1,256,128]{3,2,1,0:T(8,128)(2,1)} %all-to-all-done.1), kind=kOutput, calls=%fused_computation.1 | convolution fusion | flops 6446710784 | bytes 20971520 | tf_op jit(solution)/shard_map/tu,ruc->rtc/dot_general | solution.py:34
  247.1 2.2 slice_reduce_fusion
  249.5 2.7 %fusion.2 = bf16[64,256,128]{1,2,0:T(8,128)(2,1)} fusion(f32[64,128,256]{2,1,0:T(8,128)S(1)} %fusion, f32[64,128]{1,0:T(8,128)S(1)} %convolution_bitcast_fusion, f32[128]{0:T(128)S(1)} %fusion.8), kind=kLoop, calls=%fused_computation.4 | loop fusion | flops 6291456 | bytes 12616192 | tf_op jit(solution)/shard_map/convert_element_type | solution.py:45
  252.2 6.4 %copy.148 = bf16[64,256,128]{2,1,0:T(8,128)(2,1)} copy(bf16[64,256,128]{1,2,0:T(8,128)(2,1)} %fusion.2) | data formatting | bytes 8388608 | tf_op jit(solution)/shard_map/convert_element_type | solution.py:45
  (77 shorter events, 38.2 us)
Async XLA Ops:
  0.0 141.4 %copy-start = (f32[16,128]{1,0:T(8,128)S(1)}, f32[16,128]{1,0:T(8,128)}, u32[]{:S(2)}) copy-start(f32[16,128]{1,0:T(8,128)} %param.8) | copy-start | bytes 24580
  1.5 11.4 %all-to-all-start.2 = ((bf16[4,2,128]{2,1,0:T(2,128)(2,1)}), bf16[4,2,128]{2,1,0:T(2,128)(2,1)S(1)}, u32[]{:S(2)}, u32[]{:S(2)}) async-start(bf16[4,2,128]{2,1,0:T(2,128)(2,1)} %reshape.93), calls=%async_computation.2 | async-start | bytes 4096 | tf_op jit(solution)/shard_map/all_to_all | solution.py:58
  12.9 5.0 %copy-start.2 = (s32[4,16,128]{2,1,0:T(8,128)S(1)}, s32[4,16,128]{2,1,0:T(8,128)}, u32[]{:S(2)}) copy-start(s32[4,16,128]{2,1,0:T(8,128)} %param.7) | copy-start | bytes 98308
  12.9 52.5 %all-to-all-start = ((bf16[4,16,256,128]{3,2,0,1:T(8,128)(2,1)}), bf16[4,16,256,128]{3,2,0,1:T(8,128)(2,1)}, u32[]{:S(2)}, u32[]{:S(2)}) async-start(bf16[4,16,256,128]{3,2,0,1:T(8,128)(2,1)} %copy_convert_fusion), calls=%async_computation | async-start | bytes 8388608 | tf_op jit(solution)/shard_map/all_to_all | solution.py:57
  65.4 56.7 %all-to-all-start.3 = ((bf16[64,1,16]{2,1,0:T(2,128)(2,1)}), bf16[64,1,16]{2,1,0:T(2,128)(2,1)S(1)}, u32[]{:S(2)}, u32[]{:S(2)}) async-start(bf16[64,1,16]{2,1,0:T(2,128)(2,1)} %copy.144), calls=%async_computation.3 | async-start | bytes 65536 | tf_op jit(solution)/shard_map/all_to_all | solution.py:71
  81.6 39.9 %copy-start.1 = (bf16[4,4,4,256,128]{4,3,2,1,0:T(8,128)(2,1)}, bf16[4,4,4,256,128]{4,3,2,1,0:T(8,128)(2,1)S(1)}, u32[]{:S(2)}) copy-start(bf16[4,4,4,256,128]{4,3,2,1,0:T(8,128)(2,1)S(1)} %copy.140) | copy-start | bytes 12582916
  122.1 7.4 %all-to-all-start.4 = ((bf16[4,16,128]{2,0,1:T(4,128)(2,1)}), bf16[4,16,128]{2,0,1:T(4,128)(2,1)S(1)}, u32[]{:S(2)}, u32[]{:S(2)}) async-start(bf16[4,16,128]{2,0,1:T(4,128)(2,1)} %copy_convert_fusion.1), calls=%async_computation.4 | async-start | bytes 32768 | tf_op jit(solution)/shard_map/all_to_all | solution.py:59
  126.9 15.1 %copy-start.3 = (f32[128]{0:T(128)S(1)}, f32[128]{0:T(128)}, u32[]{:S(2)}) copy-start(f32[128]{0:T(128)} %param.9) | copy-start | bytes 1540
  129.6 107.5 %all-to-all-start.1 = ((bf16[64,1,256,128]{3,2,1,0:T(8,128)(2,1)}), bf16[64,1,256,128]{3,2,1,0:T(8,128)(2,1)}, u32[]{:S(2)}, u32[]{:S(2)}) async-start(bf16[64,1,256,128]{3,2,1,0:T(8,128)(2,1)} %constant_dynamic-update-slice_fusion), calls=%async_computation.1 | async-start | bytes 8388608 | tf_op jit(solution)/shard_map/all_to_all | solution.py:66
